TPU v7x, 128 devices: a whole 4x4x4 slice. The times are simulated.
128 devices in a mesh: row: 16 (over y, z_hi, core), col: 8 (over z_lo, x).
Axes of the slice: x: 4, y: 4, z: 4 (z_hi: 2, z_lo: 2; z = z_hi * 2 + z_lo), core: 2. Of those that a mesh axis runs over, the one named last changes fastest.
Arguments:
- vectors: float32 [32768, 8192], P('row', 'col'), may hold values from -6 to 6
- reflectors: float32 [8, 32768, 128], P('col', 'row'), may hold values from -0.03125 to 0.03125
- triangles: float32 [8, 128, 128], P('col'), may hold values from -0.25 to 1.8, as said below
Outputs:
- transformed: float32 [32768, 8192], P('row', 'col')
Inputs may be any that keep to these rules, and one draw needn't show every extreme that they name: Each triangles[p] is upper triangular with diagonal entries between 0.5 and 1.8.
All inputs are finite; a program needn't handle non-finite values.
Results may differ from a plain program's by a relative error of at most 0.00013.
Values sent between devices are 32-bit elements; how exact they have to be, the bound alone decides.
No kernel may reach another device: no remote copies, remote signals or barrier semaphores. Data moves between devices by JAX's collectives and lax.ppermute only.
A program may use at most 128 MiB of HBM per device.

v0:
```python
import jax
import jax.numpy as jnp
from jax import lax
from jax.experimental import pallas as pl
from jax.experimental.pallas import tpu as pltpu
from jax.sharding import Mesh
from jax.sharding import PartitionSpec as P

ROW = ("y", "zh", "k")
COL = ("zl", "x")
STEP = 512
F32 = jnp.float32
BF16 = jnp.bfloat16


def shifted(value, axis, by):
    peers = lax.axis_size(axis)
    return lax.ppermute(value, axis, [(i, (i + by) % peers) for i in range(peers)])


def halves(value):
    high = value.astype(BF16)
    return high, (value - high.astype(F32)).astype(BF16)


def dot(left, right, dims):
    return lax.dot_general(left, right, (dims, ((), ())), preferred_element_type=F32)


def dot_split(left, right, dims):
    (lh, ll), (rh, rl) = left, right
    (a,), (b,) = dims
    return dot(jnp.concatenate([lh, ll, lh], axis=a), jnp.concatenate([rh, rh, rl], axis=b), dims)


ROWS = ((0,), (0,))
PLAIN = ((1,), (0,))


def call(kernel, grid, ins, outs, scratch, operands, aliases=None, flops=0):
    return pl.pallas_call(
        kernel,
        grid_spec=pltpu.PrefetchScalarGridSpec(
            num_scalar_prefetch=1,
            grid=grid,
            in_specs=ins,
            out_specs=[s for s, _ in outs],
            scratch_shapes=scratch,
        ),
        out_shape=[o for _, o in outs],
        input_output_aliases=aliases or {},
        cost_estimate=pl.CostEstimate(flops=flops, bytes_accessed=flops // 256, transcendentals=0),
        compiler_params=pltpu.CompilerParams(
            dimension_semantics=("arbitrary",) * len(grid), vmem_limit_bytes=56 * 1024 * 1024
        ),
    )(*operands)


def shape(*dims, dtype=F32):
    return jax.ShapeDtypeStruct(dims, dtype)


def loaded(refs, panels, i, steps):
    at, rows = 0, []
    for p in panels:
        v = refs[at][...]
        if len(p) == 2:
            v = jnp.where(i < steps // 2, v, refs[at + 1][...])
        at += len(p)
        rows.append(v)
    return rows


def specs_of(panels, steps):
    width, half = panels[0][0].shape[1], steps // 2
    out = []
    for p in panels:
        if len(p) == 1:
            out.append(pl.BlockSpec((STEP, width), lambda i, m: (i, 0)))
        else:
            out.append(pl.BlockSpec((STEP, width), lambda i, m: (jnp.minimum(i, half - 1), 0)))
            out.append(pl.BlockSpec((STEP, width), lambda i, m: (jnp.maximum(i - half, 0), 0)))
    return out


def panel_products(meta, block, panels):
    rows, cols = block.shape
    width = panels[0][0].shape[1]
    total = width * len(panels)
    steps = rows // STEP
    flat = [part for p in panels for part in p]
    piece = cols // 8

    def kernel(m, x_ref, *refs):
        mine, theirs, hi_ref, lo_ref, acc = refs[len(flat) :]
        i = pl.program_id(0)
        whole = loaded(refs, panels, i, steps)
        v = halves(jnp.concatenate(whole, axis=1) if len(whole) > 1 else whole[0])
        hi_ref[...], lo_ref[...] = v
        product = dot_split(v, halves(x_ref[...]), ROWS)

        @pl.when(i == 0)
        def _():
            acc[...] = product

        @pl.when(i > 0)
        def _():
            acc[...] += product

        @pl.when(i == steps - 1)
        def _():
            core, y = m[0], m[1]
            for dy in range(4):
                base = lax.rem(y + dy, 4) * (2 * piece)
                mine[dy] = acc[:, pl.ds(pl.multiple_of(base + core * piece, piece), piece)]
                theirs[dy] = acc[:, pl.ds(pl.multiple_of(base + (1 - core) * piece, piece), piece)]

    ins = [pl.BlockSpec((STEP, cols), lambda i, m: (i, 0)), *specs_of(panels, steps)]
    pieces = (pl.BlockSpec((4, total, piece), lambda i, m: (0, 0, 0)), shape(4, total, piece))
    split = (pl.BlockSpec((STEP, total), lambda i, m: (i, 0)), shape(rows, total, dtype=BF16))
    return call(
        kernel, (steps,), ins, [pieces, pieces, split, split],
        [pltpu.VMEM((total, cols), F32)], (meta, block, *flat), flops=6 * rows * total * cols,
    )


def inner_products(meta, panels, tri, share):
    rows, width = panels[0][0].shape
    steps = rows // STEP
    part = width // 4
    flat = [p for panel in panels for p in panel]

    def kernel(m, *refs):
        tri_ref, out, left_own, own_both, across_both = refs[len(flat) :]
        i = pl.program_id(0)
        own, left, across, far = loaded(refs, panels, i, steps)

        @pl.when(i == 0)
        def _():
            for acc in (left_own, own_both, across_both):
                acc[...] = jnp.zeros_like(acc)

        own, left, across, far = halves(own), halves(left), halves(across), halves(far)

        def beside(a, b):
            return tuple(jnp.concatenate([u, v], axis=1) for u, v in zip(a, b))

        left_own[...] += dot_split(left, own, ROWS)
        own_both[...] += dot_split(own, beside(far, across), ROWS)
        across_both[...] += dot_split(across, beside(left, far), ROWS)

        @pl.when(i == steps - 1)
        def _():
            for y in range(4):
                r = slice(y * part, (y + 1) * part)
                out[y, 0, 0] = left_own[r]
                out[y, 0, 1] = own_both[r, :width]
                out[y, 0, 2] = own_both[r, width:]
                out[y, 1, 0] = across_both[r, :width]
                out[y, 1, 1] = across_both[r, width:]
                out[y, 1, 2] = tri_ref[r] * share

    ins = [*specs_of(panels, steps), pl.BlockSpec((width, width), lambda i, m: (0, 0))]
    dims = (4, 2, 3, part, width)
    return call(
        kernel, (steps,), ins, [(pl.BlockSpec(dims, lambda i, m: (0,) * 5), shape(*dims))],
        [pltpu.VMEM((width, width), F32)] + [pltpu.VMEM((width, 2 * width), F32)] * 2,
        (meta, *flat, tri), flops=30 * rows * width * width,
    )[0]


def coupling(meta, kept, other):
    width = kept.shape[-1]

    def kernel(m, a_ref, b_ref, g_ref, t_ref):
        def fill(low, high):
            def block(b, c):
                ref, b = (low, b) if b < 3 else (high, b - 3)
                return jnp.concatenate([ref[y, c, b] for y in range(4)], axis=0)

            def put(p, q, value):
                g_ref[p, :, pl.ds(q * width, width)] = value

            for c in range(8):
                z, x = divmod(c, 4)
                left, far, across = z * 4 + (x + 3) % 4, z * 4 + (x + 2) % 4, (1 - z) * 4 + x
                for p, q, b in ((left, c, 0), (c, far, 1), (c, across, 2), (across, left, 3), (across, far, 4)):
                    if p < q:
                        put(p, q, block(b, c))
                    elif b in (0, 3):
                        put(q, p, block(b, c).T)
                t_ref[c] = block(5, c)

        @pl.when(m[0] == 0)
        def _():
            fill(a_ref, b_ref)

        @pl.when(m[0] != 0)
        def _():
            fill(b_ref, a_ref)

    every = pl.BlockSpec(kept.shape, lambda i, m: (0,) * 5)
    outs = [
        (pl.BlockSpec((8, width, 8 * width), lambda i, m: (0, 0, 0)), shape(8, width, 8 * width)),
        (pl.BlockSpec((8, width, width), lambda i, m: (0, 0, 0)), shape(8, width, width)),
    ]
    return call(kernel, (1,), [every, every], outs, [], (meta, kept, other))


def solved(meta, sums, inner, tri):
    width = tri.shape[-1]
    cols = sums[0].shape[1]

    def kernel(m, *refs):
        parts, (g_ref, t_ref, out, w, y) = refs[: len(sums)], refs[len(sums) :]
        at = 0
        for part in parts:
            w[pl.ds(at, part.shape[0]), :] = part[...]
            at += part.shape[0]
        for p in range(7, -1, -1):
            place = pl.ds(pl.multiple_of(m[2 + p] * width, width), width)
            rest = w[place, :]
            if p < 7:
                below = (p + 1) * width
                rest = rest - dot_split(
                    halves(g_ref[p, :, below:]), halves(y[below:, :]), PLAIN
                )
            value = dot_split(halves(t_ref[p]), halves(rest), PLAIN)
            y[pl.ds(p * width, width), :] = value
            out[place, :] = value

    def whole(a):
        return pl.BlockSpec(a.shape, lambda i, m: (0,) * a.ndim)

    spec = pl.BlockSpec((8 * width, cols), lambda i, m: (0, 0))
    return call(
        kernel, (1,), [whole(a) for a in (*sums, inner, tri)], [(spec, shape(8 * width, cols))],
        [pltpu.VMEM((8 * width, cols), F32)] * 2, (meta, *sums, inner, tri), flops=8 * 8 * width * width * width * 6,
    )[0]


def updated(meta, block, bases, ys, offsets, before):
    rows, cols = block.shape
    piece = cols // 8
    order = ys[0][0].shape[0]
    flat_v = [part for b in bases for part in b]
    flat_y = [part for y in ys for part in y]

    def kernel(m, x_ref, *refs):
        n = len(flat_v)
        v_refs, y_refs, (out, hi, lo) = refs[:n], refs[n : n + len(flat_y)], refs[-3:]
        i, j = pl.program_id(0), pl.program_id(1)

        @pl.when((i == 0) & (j == 0))
        def _():
            core = m[0]
            for at in range(len(ys)):
                for half, ref in enumerate(y_refs[2 * at : 2 * at + 2]):
                    place = pl.ds(pl.multiple_of(jnp.where(half == 0, core, 1 - core) * piece, piece), piece)
                    high, low = halves(ref[...])
                    hi[at, :, place] = high
                    lo[at, :, place] = low

        high = [v_refs[2 * b][...] for b in range(len(bases))]
        low = [v_refs[2 * b + 1][...] for b in range(len(bases))]
        v = jnp.concatenate(high + low + high, axis=1)
        out[...] = x_ref[...] - dot(v, jnp.concatenate([hi[j], hi[j], lo[j]], axis=0), PLAIN)

    def where(i, j, m):
        off = jnp.int32(offsets[0])
        for at, o in enumerate(offsets[1:], 1):
            off = jnp.where(j == at, o, off)
        return i, lax.rem(m[1] + off, 4)

    ins = [pl.BlockSpec((STEP, 2 * piece), where)]
    ins += [pl.BlockSpec((STEP, v.shape[1]), lambda i, j, m: (i, 0)) for v in flat_v]
    ins += [pl.BlockSpec((order, piece), lambda i, j, m: (0, 0)) for _ in flat_y]
    operands, aliases = [meta, block, *flat_v, *flat_y], {}
    if before is not None:
        aliases = {len(operands): 0}
        ins.append(pl.BlockSpec(memory_space=pl.ANY))
        operands.append(before)
    scratch = [pltpu.VMEM((len(ys), order, 2 * piece), BF16)] * 2
    return call(
        kernel, (rows // STEP, len(ys)), ins, [(pl.BlockSpec((STEP, 2 * piece), where), shape(rows, cols))],
        scratch, operands, aliases, flops=6 * rows * order * 2 * piece * len(ys),
    )[0]


def near_sum(mine, theirs):
    both = mine + shifted(theirs, "k", 1)
    near = shifted(both[1], "y", 1), shifted(both[3], "y", -1), shifted(both[2], "y", 2)
    return both[0] + near[0] + near[1] + near[2]


def doubled(total):
    return total + shifted(total, "zh", 1)


def from_everyone(piece, axes):
    peers = lax.axis_size(axes)
    return lax.all_to_all(jnp.broadcast_to(piece[None], (peers, *piece.shape)), axes, 0, 0, tiled=True)


def shards(vectors, reflectors, triangles):
    own, tri = reflectors[0], triangles[0]
    core, y, z, x = (lax.axis_index(a) for a in ("k", "y", "zl", "x"))
    places = []
    for p in range(8):
        pz, px = divmod(p, 4)
        dx = lax.rem(px - x + 4, 4)
        same = jnp.where(dx == 0, 0, jnp.where(dx == 3, 1, jnp.where(dx == 1, 2, 4)))
        cross = jnp.where(dx == 0, 3, jnp.where(dx == 3, 5, jnp.where(dx == 1, 6, 7)))
        places.append(jnp.where(pz == z, same, cross))
    meta = jnp.stack([core, y, *places]).astype(jnp.int32)
    return body(meta, vectors, own, tri)


def body(meta, vectors, own, tri):
    half = own.shape[0] // 2
    upper, lower = own[:half], own[half:]
    left0, right1 = shifted(upper, "x", 1), shifted(lower, "x", -1)
    across = shifted(own, "zl", 1)
    left1, right0 = shifted(lower, "x", 1), shifted(upper, "x", -1)
    far = shifted(left0, "x", 1), shifted(right1, "x", -1)
    left, right = (left0, left1), (right0, right1)
    across_left, across_right = shifted(across, "x", 1), shifted(across, "x", -1)
    across_far = shifted(far[0], "zl", 1), shifted(far[1], "zl", 1)

    m0, t0, h0, l0 = panel_products(meta, vectors, [(own,)])
    sum0 = near_sum(m0, t0)
    m1, t1, h1, l1 = panel_products(meta, vectors, [left, right, (across,)])
    ginner = inner_products(meta, [(own,), left, (across,), far], tri, 1.0 / 16.0)
    parts = lax.all_to_all(ginner.reshape(8, *ginner.shape[2:]), ("y", "k"), 0, 0, tiled=True)
    gsum = jnp.sum(parts, axis=0)
    gsum = doubled(gsum)
    sum1 = near_sum(m1, t1)
    early = doubled(jnp.concatenate([sum0, sum1]))
    gall = from_everyone(gsum, ("y", "zl", "x")).reshape(4, 8, *gsum.shape)
    inner, tris = coupling(meta, gall, shifted(gall, "k", 1))
    m2, t2, h2, l2 = panel_products(meta, vectors, [far, (across_left,), (across_right,), across_far])
    late = doubled(near_sum(m2, t2))
    ys = solved(meta, (early, late), inner, tris)

    bases = (h0, l0), (h1, l1), (h2, l2)
    ahead, behind = shifted(ys, "y", -1), shifted(ys, "y", 1)
    out = updated(meta, vectors, bases, [(ys, shifted(ys, "k", 1))], (0,), None)
    top = ys.shape[0] // 2
    away = shifted(ahead[:top], "y", -1), shifted(behind[top:], "y", 1)
    side = [(v, shifted(v, "k", 1)) for v in (ahead, behind)]
    out = updated(meta, vectors, bases, side, (1, 3), out)
    away = jnp.concatenate(away)
    return updated(meta, vectors, bases, [(away, shifted(away, "k", 1))], (2,), out)


def solution(mesh):
    torus = Mesh(mesh.devices.reshape(4, 2, 2, 2, 4), ROW + COL)
    return jax.shard_map(
        shards,
        mesh=torus,
        in_specs=(P(ROW, COL), P(COL, ROW, None), P(COL, None, None)),
        out_specs=P(ROW, COL),
        check_vma=False,
    )
```

profile of v0, /device:TPU:1, one launch (start us, length us, event | category | flops | bytes accessed | tf_op | source)
XLA Modules:
  0.0 217.6 jit_solution(13870661029972969298)
XLA Ops:
  0.0 2.5 %collective-permute-start.4 = (f32[2048,128]{1,0:T(8,128)}, f32[2048,128]{1,0:T(8,128)S(1)}, u32[]{:S(2)}, u32[]{:S(2)}) collective-permute-start(f32[2048,128]{1,0:T(8,128)} %bitcast.60), channel_id=1, source_target_pairs={{0,4},{4,0},{1,5},{5,1},{2,6},{6,2},{3,7},{7,3},{8,12},{12,8},{9,1... | collective-permute-start | bytes 3145736 | tf_op jit(solution)/shard_map/ppermute | solution.py:18
  7.2 11.3 %collective-permute-done.refs_0_.refs_1_ = f32[1024,128]{1,0:T(8,128)S(1)} collective-permute-done((f32[1024,128]{1,0:T(8,128)}, f32[1024,128]{1,0:T(8,128)S(1)}, u32[]{:S(2)}, u32[]{:S(2)}) %collective-permute-start) | collective-permute-done | bytes 524320 | tf_op jit(solution)/shard_map/ppermute | solution.py:18
  18.5 2.7 %collective-permute-start.6 = (f32[1024,128]{1,0:T(8,128)S(1)}, f32[1024,128]{1,0:T(8,128)}, u32[]{:S(2)}, u32[]{:S(2)}) collective-permute-start(f32[1024,128]{1,0:T(8,128)S(1)} %collective-permute-done.3.refs_3_), channel_id=1, source_target_pairs={{0,3},{1,0},{2,1},{3,2},{4,7},{5,4},{6,5},{7,6},{8,11},{9,8},{10,9... | collective-permute-start | bytes 1572872 | tf_op jit(solution)/shard_map/ppermute | solution.py:18
  21.2 4.5 %collective-permute-done.4.refs_4_.refs_3_ = f32[2048,128]{1,0:T(8,128)S(1)} collective-permute-done((f32[2048,128]{1,0:T(8,128)}, f32[2048,128]{1,0:T(8,128)S(1)}, u32[]{:S(2)}, u32[]{:S(2)}) %collective-permute-start.4) | collective-permute-done | bytes 1048608 | tf_op jit(solution)/shard_map/ppermute | solution.py:18
  28.9 2.6 %collective-permute-done.5.refs_0_.refs_4_ = f32[1024,128]{1,0:T(8,128)} collective-permute-done((f32[1024,128]{1,0:T(8,128)S(1)}, f32[1024,128]{1,0:T(8,128)}, u32[]{:S(2)}, u32[]{:S(2)}) %collective-permute-start.5) | collective-permute-done | bytes 524320 | tf_op jit(solution)/shard_map/ppermute | solution.py:18
  32.9 9.7 %collective-permute-done.1.refs_1_.refs_2_ = f32[1024,128]{1,0:T(8,128)S(1)} collective-permute-done((f32[1024,128]{1,0:T(8,128)S(1)}, f32[1024,128]{1,0:T(8,128)S(1)}, u32[]{:S(2)}, u32[]{:S(2)}) %collective-permute-start.1) | collective-permute-done | bytes 524320 | tf_op jit(solution)/shard_map/ppermute | solution.py:18
  43.4 6.2 %shard_map.40 = f32[4,2,3,32,128]{4,3,2,1,0:T(8,128)} custom-call(s32[10]{0:T(128)} %stack.43.m, f32[2048,128]{1,0:T(8,128)} %bitcast.61, f32[1024,128]{1,0:T(8,128)} %copy-done.10, f32[1024,128]{1,0:T(8,128)} %copy-done.11, f32[2048,128]{1,0:T(8,128)} %copy-done.5, f32[1024,128]{1,0:T(8,128)} %collective-permute-done.5.refs_0_.refs_4_, ...), custom_call_target="tpu_custom_call" | custom-call | flops 1006632960 | bytes 3932160 | tf_op jit(solution)/shard_map/pallas_call | solution.py:41
  49.6 17.4 %all_to_all.10 = f32[8,3,32,128]{3,2,1,0:T(8,128)S(1)} all-to-all(f32[8,3,32,128]{3,2,1,0:T(8,128)} %bitcast.65), channel_id=1, replica_groups=mesh['y'=4,'zh'=2,'k'=2,'zl'=2,'x'=4] {'y','k'}, dimensions={0} | all-to-all | bytes 786432 | tf_op jit(solution)/shard_map/all_to_all | solution.py:334
  67.0 3.4 %collective-permute-start.25 = (f32[3,32,128]{2,1,0:T(8,128)S(1)}, f32[3,32,128]{2,1,0:T(8,128)S(1)}, u32[]{:S(2)}, u32[]{:S(2)}) collective-permute-start(f32[3,32,128]{2,1,0:T(8,128)S(1)} %reduce_sum.9), channel_id=1, source_target_pairs={{0,16},{16,0},{1,17},{17,1},{2,18},{18,2},{3,19},{19,3},{4,20},{20... | collective-permute-start | bytes 147464 | tf_op jit(solution)/shard_map/ppermute | solution.py:18
  70.4 7.2 %shard_map.37 = (f32[4,128,128]{2,1,0:T(8,128)}, f32[4,128,128]{2,1,0:T(8,128)}, bf16[2048,128]{1,0:T(8,128)(2,1)}, bf16[2048,128]{1,0:T(8,128)(2,1)}) custom-call(s32[10]{0:T(128)} %stack.43.m, f32[2048,1024]{1,0:T(8,128)} %x_ref.11, f32[2048,128]{1,0:T(8,128)} %bitcast.62), custom_call_target="tpu_custom_call" | custom-call | flops 1610612736 | bytes 6291456 | tf_op jit(solution)/shard_map/pallas_call | solution.py:41
  79.1 4.0 %all-to-all-start.1 = ((f32[32,3,32,128]{3,2,1,0:T(8,128)}), f32[32,3,32,128]{3,2,1,0:T(8,128)S(1)}, u32[]{:S(2)}, u32[]{:S(2)}) async-start(f32[32,3,32,128]{3,2,1,0:T(8,128)} %broadcast_in_dim.2), calls=%async_computation.1 | async-start | bytes 3145728 | tf_op jit(solution)/shard_map/all_to_all | solution.py:302
  84.6 13.0 %shard_map.39 = (f32[4,512,128]{2,1,0:T(8,128)}, f32[4,512,128]{2,1,0:T(8,128)}, bf16[2048,512]{1,0:T(8,128)(2,1)}, bf16[2048,512]{1,0:T(8,128)(2,1)}) custom-call(s32[10]{0:T(128)} %stack.43.m, f32[2048,1024]{1,0:T(8,128)} %x_ref.11, f32[1024,128]{1,0:T(8,128)} %collective-permute-done.5.refs_0_.refs_4_, ...), custom_call_target="tpu_custom_call" | custom-call | flops 6442450944 | bytes 25165824 | tf_op jit(solution)/shard_map/pallas_call | solution.py:41
  98.6 11.1 %shard_map.38 = (f32[4,384,128]{2,1,0:T(8,128)}, f32[4,384,128]{2,1,0:T(8,128)}, bf16[2048,384]{1,0:T(8,128)(2,1)}, bf16[2048,384]{1,0:T(8,128)(2,1)}) custom-call(s32[10]{0:T(128)} %stack.43.m, f32[2048,1024]{1,0:T(8,128)} %x_ref.11, f32[1024,128]{1,0:T(8,128)} %copy-done.10, f32[1024,128]{1,0:T(8,128)} %copy-done.11, f32[1024,128]{1,0:T(8,128)} %copy-done.15, ...), custom_call_target="tpu_custom_call" | custom-call | flops 4831838208 | bytes 18874368 | tf_op jit(solution)/shard_map/pallas_call | solution.py:41
  130.6 7.2 %collective-permute-done.21 = f32[512,128]{1,0:T(8,128)S(1)} collective-permute-done((f32[512,128]{1,0:T(8,128)S(1)}, f32[512,128]{1,0:T(8,128)S(1)}, u32[]{:S(2)}, u32[]{:S(2)}) %collective-permute-start.21) | collective-permute-done | bytes 262176 | tf_op jit(solution)/shard_map/ppermute | solution.py:18
  137.8 3.9 %collective-permute-done.23 = f32[512,128]{1,0:T(8,128)S(1)} collective-permute-done((f32[512,128]{1,0:T(8,128)S(1)}, f32[512,128]{1,0:T(8,128)S(1)}, u32[]{:S(2)}, u32[]{:S(2)}) %collective-permute-start.23) | collective-permute-done | bytes 262176 | tf_op jit(solution)/shard_map/ppermute | solution.py:18
  142.5 6.9 %collective-permute-done.24 = f32[512,128]{1,0:T(8,128)S(1)} collective-permute-done((f32[512,128]{1,0:T(8,128)S(1)}, f32[512,128]{1,0:T(8,128)S(1)}, u32[]{:S(2)}, u32[]{:S(2)}) %collective-permute-start.24) | collective-permute-done | bytes 262176 | tf_op jit(solution)/shard_map/ppermute | solution.py:18
  151.3 5.0 %shard_map.41 = (f32[8,128,1024]{2,1,0:T(8,128)}, f32[8,128,128]{2,1,0:T(8,128)}) custom-call(s32[10]{0:T(128)} %stack.43.m, f32[4,8,3,32,128]{4,3,2,1,0:T(8,128)} %bitcast.64, f32[4,8,3,32,128]{4,3,2,1,0:T(8,128)} %copy-done.1), custom_call_target="tpu_custom_call" | custom-call | tf_op jit(solution)/shard_map/pallas_call | solution.py:41
  156.3 7.0 %shard_map.42.refs_6_ = f32[1024,128]{1,0:T(8,128)} custom-call(s32[10]{0:T(128)} %stack.43.m, f32[512,128]{1,0:T(8,128)} %fusion.9.refs_0_, f32[512,128]{1,0:T(8,128)} %add.82.refs_1_, f32[8,128,1024]{2,1,0:T(8,128)} %get-tuple-element.31.refs_2_, f32[8,128,128]{2,1,0:T(8,128)} %get-tuple-element.32.refs_3_), custom_call_target="tpu_custom_call" | custom-call | flops 805306368 | bytes 3145728 | tf_op jit(solution)/shard_map/pallas_call | solution.py:41
  164.8 3.5 %collective-permute-start.34 = (f32[1024,128]{1,0:T(8,128)}, f32[1024,128]{1,0:T(8,128)S(1)}, u32[]{:S(2)}, u32[]{:S(2)}) collective-permute-start(f32[1024,128]{1,0:T(8,128)} %shard_map.42.refs_6_), channel_id=1, source_target_pairs={{0,8},{8,0},{1,9},{9,1},{2,10},{10,2},{3,11},{11,3},{4,12},{12,4},... | collective-permute-start | bytes 1572872 | tf_op jit(solution)/shard_map/ppermute | solution.py:18
  168.3 6.1 %collective-permute-done.27.refs_6_ = f32[1024,128]{1,0:T(8,128)S(1)} collective-permute-done((f32[1024,128]{1,0:T(8,128)}, f32[1024,128]{1,0:T(8,128)S(1)}, u32[]{:S(2)}, u32[]{:S(2)}) %collective-permute-start.27) | collective-permute-done | bytes 524320 | tf_op jit(solution)/shard_map/ppermute | solution.py:18
  176.1 4.3 %collective-permute-start.32 = (f32[1024,128]{1,0:T(8,128)S(1)}, f32[1024,128]{1,0:T(8,128)S(1)}, u32[]{:S(2)}, u32[]{:S(2)}) collective-permute-start(f32[1024,128]{1,0:T(8,128)S(1)} %collective-permute-done.27.refs_6_), channel_id=1, source_target_pairs={{0,8},{8,0},{1,9},{9,1},{2,10},{10,2},{3,11},{11,3},{4,12},{12,4},... | collective-permute-start | bytes 1572872 | tf_op jit(solution)/shard_map/ppermute | solution.py:18
  181.2 9.1 %shard_map.43.refs_10_ = f32[2048,1024]{1,0:T(8,128)} custom-call(s32[10]{0:T(128)} %stack.43.m, f32[2048,1024]{1,0:T(8,128)} %x_ref.11, bf16[2048,128]{1,0:T(8,128)(2,1)} %get-tuple-element.19.refs_0_, bf16[2048,128]{1,0:T(8,128)(2,1)} %get-tuple-element.20.refs_1_, bf16[2048,384]{1,0:T(8,128)(2,1)} %get-tuple-element.21.refs_2_, ...), custom_call_target="tpu_custom_call" | custom-call | flops 3221225472 | bytes 12582912 | tf_op jit(solution)/shard_map/pallas_call | solution.py:41
  192.6 15.0 %shard_map.44.refs_8_ = f32[2048,1024]{1,0:T(8,128)} custom-call(s32[10]{0:T(128)} %stack.43.m, f32[2048,1024]{1,0:T(8,128)} %x_ref.11, bf16[2048,128]{1,0:T(8,128)(2,1)} %get-tuple-element.19.refs_0_, bf16[2048,128]{1,0:T(8,128)(2,1)} %get-tuple-element.20.refs_1_, bf16[2048,384]{1,0:T(8,128)(2,1)} %get-tuple-element.21.refs_2_, ...), custom_call_target="tpu_custom_call", output_to_operand_aliasing={{}: (12, {})} | custom-call | flops 6442450944 | bytes 25165824 | tf_op jit(solution)/shard_map/pallas_call | solution.py:41
  208.4 9.1 %shard_map.45 = f32[2048,1024]{1,0:T(8,128)} custom-call(s32[10]{0:T(128)} %stack.43.m, f32[2048,1024]{1,0:T(8,128)} %x_ref.11, bf16[2048,128]{1,0:T(8,128)(2,1)} %get-tuple-element.19.refs_0_, bf16[2048,128]{1,0:T(8,128)(2,1)} %get-tuple-element.20.refs_1_, bf16[2048,384]{1,0:T(8,128)(2,1)} %get-tuple-element.21.refs_2_, ...), custom_call_target="tpu_custom_call", output_to_operand_aliasing={{}: (10, {})} | custom-call | flops 3221225472 | bytes 12582912 | tf_op jit(solution)/shard_map/pallas_call | solution.py:41
  (113 shorter events, 44.8 us)
Async XLA Ops:
  0.0 25.6 %collective-permute-start.4 = (f32[2048,128]{1,0:T(8,128)}, f32[2048,128]{1,0:T(8,128)S(1)}, u32[]{:S(2)}, u32[]{:S(2)}) collective-permute-start(f32[2048,128]{1,0:T(8,128)} %bitcast.60), channel_id=1, source_target_pairs={{0,4},{4,0},{1,5},{5,1},{2,6},{6,2},{3,7},{7,3},{8,12},{12,8},{9,1... | collective-permute-start | bytes 3145736 | tf_op jit(solution)/shard_map/ppermute | solution.py:18
  4.5 13.9 %collective-permute-start = (f32[1024,128]{1,0:T(8,128)}, f32[1024,128]{1,0:T(8,128)S(1)}, u32[]{:S(2)}, u32[]{:S(2)}) collective-permute-start(f32[1024,128]{1,0:T(8,128)} %get-tuple-element.37), channel_id=1, source_target_pairs={{0,1},{1,2},{2,3},{3,0},{4,5},{5,6},{6,7},{7,4},{8,9},{9,10},{10,1... | collective-permute-start | bytes 1572872 | tf_op jit(solution)/shard_map/ppermute | solution.py:18
  5.7 12.7 %collective-permute-start.3 = (f32[1024,128]{1,0:T(8,128)S(1)}, f32[1024,128]{1,0:T(8,128)S(1)}, u32[]{:S(2)}, u32[]{:S(2)}) collective-permute-start(f32[1024,128]{1,0:T(8,128)S(1)} %get-tuple-element.36), channel_id=1, source_target_pairs={{0,3},{1,0},{2,1},{3,2},{4,7},{5,4},{6,5},{7,6},{8,11},{9,8},{10,9... | collective-permute-start | bytes 1572872 | tf_op jit(solution)/shard_map/ppermute | solution.py:18
  18.5 13.0 %collective-permute-start.5 = (f32[1024,128]{1,0:T(8,128)S(1)}, f32[1024,128]{1,0:T(8,128)}, u32[]{:S(2)}, u32[]{:S(2)}) collective-permute-start(f32[1024,128]{1,0:T(8,128)S(1)} %collective-permute-done.refs_0_.refs_1_), channel_id=1, source_target_pairs={{0,1},{1,2},{2,3},{3,0},{4,5},{5,6},{6,7},{7,4},{8,9},{9,10},{10,1... | collective-permute-start | bytes 1572872 | tf_op jit(solution)/shard_map/ppermute | solution.py:18
  18.5 13.5 %collective-permute-start.6 = (f32[1024,128]{1,0:T(8,128)S(1)}, f32[1024,128]{1,0:T(8,128)}, u32[]{:S(2)}, u32[]{:S(2)}) collective-permute-start(f32[1024,128]{1,0:T(8,128)S(1)} %collective-permute-done.3.refs_3_), channel_id=1, source_target_pairs={{0,3},{1,0},{2,1},{3,2},{4,7},{5,4},{6,5},{7,6},{8,11},{9,8},{10,9... | collective-permute-start | bytes 1572872 | tf_op jit(solution)/shard_map/ppermute | solution.py:18
  21.1 21.4 %collective-permute-start.1 = (f32[1024,128]{1,0:T(8,128)S(1)}, f32[1024,128]{1,0:T(8,128)S(1)}, u32[]{:S(2)}, u32[]{:S(2)}) collective-permute-start(f32[1024,128]{1,0:T(8,128)S(1)} %get-tuple-element.36), channel_id=1, source_target_pairs={{0,1},{1,2},{2,3},{3,0},{4,5},{5,6},{6,7},{7,4},{8,9},{9,10},{10,1... | collective-permute-start | bytes 1572872 | tf_op jit(solution)/shard_map/ppermute | solution.py:18
  25.6 59.0 %collective-permute-start.7 = (f32[2048,128]{1,0:T(8,128)S(1)}, f32[2048,128]{1,0:T(8,128)}, u32[]{:S(2)}, u32[]{:S(2)}) collective-permute-start(f32[2048,128]{1,0:T(8,128)S(1)} %collective-permute-done.4.refs_4_.refs_3_), channel_id=1, source_target_pairs={{0,1},{1,2},{2,3},{3,0},{4,5},{5,6},{6,7},{7,4},{8,9},{9,10},{10,1... | collective-permute-start | bytes 3145736 | tf_op jit(solution)/shard_map/ppermute | solution.py:18
  26.7 57.9 %collective-permute-start.8 = (f32[2048,128]{1,0:T(8,128)S(1)}, f32[2048,128]{1,0:T(8,128)}, u32[]{:S(2)}, u32[]{:S(2)}) collective-permute-start(f32[2048,128]{1,0:T(8,128)S(1)} %collective-permute-done.4.refs_4_.refs_3_), channel_id=1, source_target_pairs={{0,3},{1,0},{2,1},{3,2},{4,7},{5,4},{6,5},{7,6},{8,11},{9,8},{10,9... | collective-permute-start | bytes 3145736 | tf_op jit(solution)/shard_map/ppermute | solution.py:18
  31.5 51.7 %collective-permute-start.9 = (f32[1024,128]{1,0:T(8,128)}, f32[1024,128]{1,0:T(8,128)}, u32[]{:S(2)}, u32[]{:S(2)}) collective-permute-start(f32[1024,128]{1,0:T(8,128)} %collective-permute-done.5.refs_0_.refs_4_), channel_id=1, source_target_pairs={{0,4},{4,0},{1,5},{5,1},{2,6},{6,2},{3,7},{7,3},{8,12},{12,8},{9,1... | collective-permute-start | bytes 1572872 | tf_op jit(solution)/shard_map/ppermute | solution.py:18
  32.0 52.6 %collective-permute-start.10 = (f32[1024,128]{1,0:T(8,128)}, f32[1024,128]{1,0:T(8,128)}, u32[]{:S(2)}, u32[]{:S(2)}) collective-permute-start(f32[1024,128]{1,0:T(8,128)} %collective-permute-done.6.refs_1_.refs_5_), channel_id=1, source_target_pairs={{0,4},{4,0},{1,5},{5,1},{2,6},{6,2},{3,7},{7,3},{8,12},{12,8},{9,1... | collective-permute-start | bytes 1572872 | tf_op jit(solution)/shard_map/ppermute | solution.py:18
  77.6 20.1 %collective-permute-start.2 = (f32[1024,128]{1,0:T(8,128)}, f32[1024,128]{1,0:T(8,128)S(1)}, u32[]{:S(2)}, u32[]{:S(2)}) collective-permute-start(f32[1024,128]{1,0:T(8,128)} %get-tuple-element.37), channel_id=1, source_target_pairs={{0,3},{1,0},{2,1},{3,2},{4,7},{5,4},{6,5},{7,6},{8,11},{9,8},{10,9... | collective-permute-start | bytes 1572872 | tf_op jit(solution)/shard_map/ppermute | solution.py:18
  79.1 36.2 %all-to-all-start.1 = ((f32[32,3,32,128]{3,2,1,0:T(8,128)}), f32[32,3,32,128]{3,2,1,0:T(8,128)S(1)}, u32[]{:S(2)}, u32[]{:S(2)}) async-start(f32[32,3,32,128]{3,2,1,0:T(8,128)} %broadcast_in_dim.2), calls=%async_computation.1 | async-start | bytes 3145728 | tf_op jit(solution)/shard_map/all_to_all | solution.py:302
  83.1 27.1 %collective-permute-start.11 = (f32[4,128,128]{2,1,0:T(8,128)S(1)}, f32[4,128,128]{2,1,0:T(8,128)S(1)}, u32[]{:S(2)}, u32[]{:S(2)}) collective-permute-start(f32[4,128,128]{2,1,0:T(8,128)S(1)} %copy-done.16), channel_id=1, source_target_pairs={{0,8},{8,0},{1,9},{9,1},{2,10},{10,2},{3,11},{11,3},{4,12},{12,4},... | collective-permute-start | bytes 786440 | tf_op jit(solution)/shard_map/ppermute | solution.py:18
  97.6 24.9 %collective-permute-start.20 = (f32[4,512,128]{2,1,0:T(8,128)}, f32[4,512,128]{2,1,0:T(8,128)}, u32[]{:S(2)}, u32[]{:S(2)}) collective-permute-start(f32[4,512,128]{2,1,0:T(8,128)} %get-tuple-element.30), channel_id=1, source_target_pairs={{0,8},{8,0},{1,9},{9,1},{2,10},{10,2},{3,11},{11,3},{4,12},{12,4},... | collective-permute-start | bytes 3145736 | tf_op jit(solution)/shard_map/ppermute | solution.py:18
  115.3 34.8 %collective-permute-start.26 = (f32[4,8,3,32,128]{4,3,2,1,0:T(8,128)S(1)}, f32[4,8,3,32,128]{4,3,2,1,0:T(8,128)S(1)}, u32[]{:S(2)}, u32[]{:S(2)}) collective-permute-start(f32[4,8,3,32,128]{4,3,2,1,0:T(8,128)S(1)} %bitcast.63), channel_id=1, source_target_pairs={{0,8},{8,0},{1,9},{9,1},{2,10},{10,2},{3,11},{11,3},{4,12},{12,4},... | collective-permute-start | bytes 4718600 | tf_op jit(solution)/shard_map/ppermute | solution.py:18
  123.9 13.9 %collective-permute-start.21 = (f32[512,128]{1,0:T(8,128)S(1)}, f32[512,128]{1,0:T(8,128)S(1)}, u32[]{:S(2)}, u32[]{:S(2)}) collective-permute-start(f32[512,128]{1,0:T(8,128)S(1)} %get-tuple-element.33), channel_id=1, source_target_pairs={{0,32},{32,64},{64,96},{96,0},{1,33},{33,65},{65,97},{97,1},{2,34}... | collective-permute-start | bytes 786440 | tf_op jit(solution)/shard_map/ppermute | solution.py:18
  125.5 12.3 %collective-permute-start.22 = (f32[512,128]{1,0:T(8,128)S(1)}, f32[512,128]{1,0:T(8,128)S(1)}, u32[]{:S(2)}, u32[]{:S(2)}) collective-permute-start(f32[512,128]{1,0:T(8,128)S(1)} %get-tuple-element.35), channel_id=1, source_target_pairs={{0,96},{32,0},{64,32},{96,64},{1,97},{33,1},{65,33},{97,65},{2,98}... | collective-permute-start | bytes 786440 | tf_op jit(solution)/shard_map/ppermute | solution.py:18
  126.7 15.0 %collective-permute-start.23 = (f32[512,128]{1,0:T(8,128)S(1)}, f32[512,128]{1,0:T(8,128)S(1)}, u32[]{:S(2)}, u32[]{:S(2)}) collective-permute-start(f32[512,128]{1,0:T(8,128)S(1)} %get-tuple-element.34), channel_id=1, source_target_pairs={{0,64},{32,96},{64,0},{96,32},{1,65},{33,97},{65,1},{97,33},{2,66}... | collective-permute-start | bytes 786440 | tf_op jit(solution)/shard_map/ppermute | solution.py:18
  130.5 11.3 %collective-permute-start.19 = (f32[512,128]{1,0:T(8,128)S(1)}, f32[512,128]{1,0:T(8,128)S(1)}, u32[]{:S(2)}, u32[]{:S(2)}) collective-permute-start(f32[512,128]{1,0:T(8,128)S(1)} %pad_maximum_fusion), channel_id=1, source_target_pairs={{0,16},{16,0},{1,17},{17,1},{2,18},{18,2},{3,19},{19,3},{4,20},{20... | collective-permute-start | bytes 786440 | tf_op jit(solution)/shard_map/ppermute | solution.py:18
  164.8 15.6 %collective-permute-start.34 = (f32[1024,128]{1,0:T(8,128)}, f32[1024,128]{1,0:T(8,128)S(1)}, u32[]{:S(2)}, u32[]{:S(2)}) collective-permute-start(f32[1024,128]{1,0:T(8,128)} %shard_map.42.refs_6_), channel_id=1, source_target_pairs={{0,8},{8,0},{1,9},{9,1},{2,10},{10,2},{3,11},{11,3},{4,12},{12,4},... | collective-permute-start | bytes 1572872 | tf_op jit(solution)/shard_map/ppermute | solution.py:18
  174.4 15.9 %collective-permute-start.28 = (f32[512,128]{1,0:T(8,128)S(1)}, f32[512,128]{1,0:T(8,128)S(1)}, u32[]{:S(2)}, u32[]{:S(2)}) collective-permute-start(f32[512,128]{1,0:T(8,128)S(1)} %slice.84), channel_id=1, source_target_pairs={{0,96},{32,0},{64,32},{96,64},{1,97},{33,1},{65,33},{97,65},{2,98}... | collective-permute-start | bytes 786440 | tf_op jit(solution)/shard_map/ppermute | solution.py:18
  174.6 15.8 %collective-permute-start.30 = (f32[512,128]{1,0:T(8,128)S(1)}, f32[512,128]{1,0:T(8,128)S(1)}, u32[]{:S(2)}, u32[]{:S(2)}) collective-permute-start(f32[512,128]{1,0:T(8,128)S(1)} %slice.85), channel_id=1, source_target_pairs={{0,32},{32,64},{64,96},{96,0},{1,33},{33,65},{65,97},{97,1},{2,34}... | collective-permute-start | bytes 786440 | tf_op jit(solution)/shard_map/ppermute | solution.py:18
  176.1 14.9 %collective-permute-start.32 = (f32[1024,128]{1,0:T(8,128)S(1)}, f32[1024,128]{1,0:T(8,128)S(1)}, u32[]{:S(2)}, u32[]{:S(2)}) collective-permute-start(f32[1024,128]{1,0:T(8,128)S(1)} %collective-permute-done.27.refs_6_), channel_id=1, source_target_pairs={{0,8},{8,0},{1,9},{9,1},{2,10},{10,2},{3,11},{11,3},{4,12},{12,4},... | collective-permute-start | bytes 1572872 | tf_op jit(solution)/shard_map/ppermute | solution.py:18
  190.4 17.2 %collective-permute-start.31 = (f32[1024,128]{1,0:T(8,128)S(1)}, f32[1024,128]{1,0:T(8,128)S(1)}, u32[]{:S(2)}, u32[]{:S(2)}) collective-permute-start(f32[1024,128]{1,0:T(8,128)S(1)} %constant_dynamic-update-slice_fusion.refs_6_), channel_id=1, source_target_pairs={{0,8},{8,0},{1,9},{9,1},{2,10},{10,2},{3,11},{11,3},{4,12},{12,4},... | collective-permute-start | bytes 1572872 | tf_op jit(solution)/shard_map/ppermute | solution.py:18
  (29 other events, 288.1 us)
where the time goes:
time: 219 us; the launch traced here: 218 us
  Pallas kernels  82.8 us (38%)
  waiting for transfers between devices  57.9 us (26%)
  starting transfers between devices  44.5 us (20%)
  blocking collectives  17.4 us (8%)
  local copies, waits for them, and re-layouts  10.2 us (5%)
  other arithmetic  4.43 us (2%)
    pallas_call x9, Pallas kernels, call(): pl.pallas_call(kernel, grid_spec=pltpu.PrefetchScalarGridSpec(num_scalar_...  82.8 us
    ppermute x35, waiting for transfers between devices, shifted(): lax.ppermute(value, axis, [(i, (i + by) % peers) for i in range(peers)])  57.9 us
    ppermute x35, starting transfers between devices, shifted(): lax.ppermute(value, axis, [(i, (i + by) % peers) for i in range(peers)])  40.6 us
    all_to_all x1, blocking collectives, body(): lax.all_to_all(ginner.reshape(8, *ginner.shape[2:]), ('y', 'k'), 0, 0, ti...  17.4 us
    unnamed x35, local copies, waits for them, and re-layouts  6.07 us
  transfers between devices with their start and end apart: 36, of which 12 were waited for; matrix products, arithmetic and copies ran while one was open for 4% of the time, Pallas kernels for 28%

commit v1 on v0

v1 whole, which is shorter than its diff:
```python
import jax
import jax.numpy as jnp
from jax import lax
from jax.experimental import pallas as pl
from jax.experimental.pallas import tpu as pltpu
from jax.sharding import Mesh
from jax.sharding import PartitionSpec as P

ROW = ("y", "zh", "k")
COL = ("zl", "x")
STEP = 512
WIDE = 512
F32 = jnp.float32
BF16 = jnp.bfloat16


def shifted(value, axis, by):
    peers = lax.axis_size(axis)
    return lax.ppermute(value, axis, [(i, (i + by) % peers) for i in range(peers)])


def halves(value):
    high = value.astype(BF16)
    return high, (value - high.astype(F32)).astype(BF16)


def dot(left, right, dims):
    return lax.dot_general(left, right, (dims, ((), ())), preferred_element_type=F32)


def dot_split(left, right, dims):
    (lh, ll), (rh, rl) = left, right
    (a,), (b,) = dims
    return dot(jnp.concatenate([lh, ll, lh], axis=a), jnp.concatenate([rh, rh, rl], axis=b), dims)


ROWS = ((0,), (0,))
PLAIN = ((1,), (0,))


def call(kernel, grid, ins, outs, scratch, operands, aliases=None, flops=0):
    return pl.pallas_call(
        kernel,
        grid_spec=pltpu.PrefetchScalarGridSpec(
            num_scalar_prefetch=1,
            grid=grid,
            in_specs=ins,
            out_specs=[s for s, _ in outs],
            scratch_shapes=scratch,
        ),
        out_shape=[o for _, o in outs],
        input_output_aliases=aliases or {},
        cost_estimate=pl.CostEstimate(flops=flops, bytes_accessed=flops // 256, transcendentals=0),
        compiler_params=pltpu.CompilerParams(
            dimension_semantics=("arbitrary",) * len(grid), vmem_limit_bytes=20 * 1024 * 1024
        ),
    )(*operands)


def onchip(*dims, dtype=F32):
    return pl.BlockSpec(memory_space=pltpu.VMEM), pltpu.VMEM(dims, dtype)


ONCHIP = pl.BlockSpec(memory_space=pltpu.VMEM)


def held(meta, block):
    rows, cols = block.shape

    def kernel(m, x_ref, high, low):
        here = pl.ds(pl.multiple_of(pl.program_id(0) * STEP, STEP), STEP)
        high[here, :], low[here, :] = halves(x_ref[...])

    ins = [pl.BlockSpec((STEP, cols), lambda i, m: (i, 0))]
    return call(kernel, (rows // STEP,), ins, [onchip(rows, cols, dtype=BF16)] * 2, [], (meta, block))


def resident(value):
    return pltpu.with_memory_space_constraint(value, pltpu.VMEM)


def shape(*dims, dtype=F32):
    return jax.ShapeDtypeStruct(dims, dtype)


def loaded(refs, panels, i, steps):
    at, rows = 0, []
    for p in panels:
        v = refs[at][...]
        if len(p) == 2:
            v = jnp.where(i < steps // 2, v, refs[at + 1][...])
        at += len(p)
        rows.append(v)
    return rows


def specs_of(panels, steps):
    width, half = panels[0][0].shape[1], steps // 2
    out = []
    for p in panels:
        if len(p) == 1:
            out.append(pl.BlockSpec((STEP, width), lambda i, m: (i, 0)))
        else:
            out.append(pl.BlockSpec((STEP, width), lambda i, m: (jnp.minimum(i, half - 1), 0)))
            out.append(pl.BlockSpec((STEP, width), lambda i, m: (jnp.maximum(i - half, 0), 0)))
    return out


def panel_products(meta, block, panels):
    rows, cols = block[0].shape
    width = panels[0][0].shape[1]
    total = width * len(panels)
    steps = rows // STEP
    flat = [part for p in panels for part in p]
    piece = cols // 8

    def kernel(m, xh_ref, xl_ref, *refs):
        mine, theirs, hi_ref, lo_ref, acc = refs[len(flat) :]
        i = pl.program_id(0)
        whole = loaded(refs, panels, i, steps)
        v = halves(jnp.concatenate(whole, axis=1) if len(whole) > 1 else whole[0])
        here = pl.ds(pl.multiple_of(i * STEP, STEP), STEP)
        hi_ref[here, :], lo_ref[here, :] = v
        product = dot_split(v, (xh_ref[here, :], xl_ref[here, :]), ROWS)

        @pl.when(i == 0)
        def _():
            acc[...] = product

        @pl.when(i > 0)
        def _():
            acc[...] += product

        @pl.when(i == steps - 1)
        def _():
            core, y = m[0], m[1]
            for dy in range(4):
                base = lax.rem(y + dy, 4) * (2 * piece)
                mine[dy] = acc[:, pl.ds(pl.multiple_of(base + core * piece, piece), piece)]
                theirs[dy] = acc[:, pl.ds(pl.multiple_of(base + (1 - core) * piece, piece), piece)]

    ins = [ONCHIP, ONCHIP, *specs_of(panels, steps)]
    pieces = (pl.BlockSpec((4, total, piece), lambda i, m: (0, 0, 0)), shape(4, total, piece))
    split = onchip(rows, total, dtype=BF16)
    return call(
        kernel, (steps,), ins, [pieces, pieces, split, split],
        [pltpu.VMEM((total, cols), F32)], (meta, *map(resident, block), *flat), flops=6 * rows * total * cols,
    )


def inner_products(meta, panels, kept, sent_on):
    rows, width = panels[0][0].shape
    steps = rows // STEP
    deep = kept.shape[1]
    half = width // 2
    flat = [p for panel in panels for p in panel]

    def kernel(m, *refs):
        kept_ref, sent_ref, mine, theirs, sums = refs[len(flat) :]
        i = pl.program_id(0)
        own, left, across, far = loaded(refs, panels, i, steps)
        firsts = m[2] < 2, m[3] == 0, m[3] != 0

        @pl.when(i == 0)
        def _():
            sums[...] = jnp.zeros_like(sums)
            for dy in range(4):
                mine[dy * deep : (dy + 1) * deep] = kept_ref[dy]
                theirs[dy * deep : (dy + 1) * deep] = sent_ref[dy]

        sums[0] += dot_split(halves(left), halves(own), ROWS)
        sums[1] += dot_split(halves(across), halves(left), ROWS)
        for at, (first, a, b) in enumerate(zip(firsts, (own, own, across), (far, across, far)), 2):
            upper, lower = jnp.where(first, a, b), jnp.where(first, b, a)
            sums[at] += dot_split(halves(upper), halves(lower), ROWS)

        def fill(low, high):
            end = 4 * deep
            starts = [pl.multiple_of(jnp.where(first, 0, half), half) for first in firsts]
            low[end : end + width] = sums[0]
            high[end : end + width] = sums[1]
            low[end + width : end + width + half] = sums[2, pl.ds(starts[0], half), :]
            high[end + width : end + width + half] = sums[4, pl.ds(starts[2], half), :]
            shared = sums[3, pl.ds(starts[1], half), :]
            low[end + width + half :] = shared[: half // 2]
            high[end + width + half :] = shared[half // 2 :]

        @pl.when((i == steps - 1) & (m[0] == 0))
        def _():
            fill(mine, theirs)

        @pl.when((i == steps - 1) & (m[0] != 0))
        def _():
            fill(theirs, mine)

    ins = [*specs_of(panels, steps), ONCHIP, ONCHIP]
    dims = (4 * deep + width + half + half // 2, width)
    out = (pl.BlockSpec(dims, lambda i, m: (0, 0)), shape(*dims))
    return call(
        kernel, (steps,), ins, [out, out], [pltpu.VMEM((5, width, width), F32)],
        (meta, *flat, kept, sent_on), flops=30 * rows * width * width,
    )


def coupling(meta, kept, other):
    width = kept.shape[-1]
    half = width // 2

    def kernel(m, a_ref, b_ref, gh, gl, th, tl):
        def put(p, q, start, value):
            r = slice(p * width + start, p * width + start + value.shape[0])
            gh[q, r], gl[q, r] = halves(value)

        def fill(low, high):
            for c in range(8):
                z, x = divmod(c, 4)
                left, far, across = z * 4 + (x + 3) % 4, z * 4 + (x + 2) % 4, (1 - z) * 4 + x
                for p, q, ref in ((left, c, low), (across, left, high)):
                    value = ref[c, :width]
                    put(min(p, q), max(p, q), 0, value if p < q else value.T)
                for p, q, ref in ((c, far, low), (across, far, high)):
                    start = 0 if p < q else half
                    put(min(p, q), max(p, q), start, ref[c, width : width + half])
                start = 0 if c < across else half
                for at, ref in enumerate((low, high)):
                    begin = width + half
                    value = ref[c, begin : begin + half // 2]
                    put(min(c, across), max(c, across), start + at * (half // 2), value)
                    begin += half // 2
                    r = slice(at * half, (at + 1) * half)
                    th[c, r], tl[c, r] = halves(ref[c, begin : begin + half])

        @pl.when(m[0] == 0)
        def _():
            fill(a_ref, b_ref)

        @pl.when(m[0] != 0)
        def _():
            fill(b_ref, a_ref)

    outs = [onchip(8, 8 * width, width, dtype=BF16)] * 2 + [onchip(8, width, width, dtype=BF16)] * 2
    return call(kernel, (1,), [ONCHIP, ONCHIP], outs, [], (meta, kept, other))


def solved(meta, sums, inner):
    width = inner[2].shape[-1]
    cols = sums[0].shape[1]

    def kernel(m, *refs):
        parts, (gh, gl, th, tl, out, w, rest) = refs[: len(sums)], refs[len(sums) :]
        at = 0
        for part in parts:
            depth = part.shape[0] // width * width
            w[pl.ds(at, depth), :] = part[:depth, :]
            at += depth
        places = [pl.ds(pl.multiple_of(m[4 + p] * width, width), width) for p in range(8)]
        for p in range(8):
            rest[pl.ds(p * width, width), :] = w[places[p], :]
        for p in range(7, -1, -1):
            value = dot_split((th[p], tl[p]), halves(rest[pl.ds(p * width, width), :]), PLAIN)
            out[places[p], :] = value
            if p:
                above = pl.ds(0, p * width)
                rest[above, :] -= dot_split((gh[p, above], gl[p, above]), halves(value), PLAIN)

    spec = pl.BlockSpec((8 * width, cols), lambda i, m: (0, 0))
    return call(
        kernel, (1,), [ONCHIP] * (len(sums) + 4), [(spec, shape(8 * width, cols))],
        [pltpu.VMEM((8 * width, cols), F32)] * 2, (meta, *sums, *map(resident, inner)), flops=8 * 8 * width * width * width * 6,
    )[0]


def updated(meta, block, bases, ys, offsets, before):
    rows, cols = block.shape
    piece = cols // 8
    order = ys[0][0].shape[0]
    flat_v = [part for b in bases for part in b]
    flat_y = [part for y in ys for part in y]

    def kernel(m, x_ref, *refs):
        n = len(flat_v)
        v_refs, y_refs, (out, hi, lo) = refs[:n], refs[n : n + len(flat_y)], refs[-3:]
        i, j = pl.program_id(0), pl.program_id(1)

        @pl.when((i == 0) & (j == 0))
        def _():
            core = m[0]
            for at in range(len(ys)):
                for half, ref in enumerate(y_refs[2 * at : 2 * at + 2]):
                    place = pl.ds(pl.multiple_of(jnp.where(half == 0, core, 1 - core) * piece, piece), piece)
                    high, low = halves(ref[...])
                    hi[at, :, place] = high
                    lo[at, :, place] = low

        here = pl.ds(pl.multiple_of(i * WIDE, WIDE), WIDE)
        high = [v_refs[2 * b][here, :] for b in range(len(bases))]
        low = [v_refs[2 * b + 1][here, :] for b in range(len(bases))]
        v = jnp.concatenate(high + low + high, axis=1)
        out[...] = x_ref[...] - dot(v, jnp.concatenate([hi[j], hi[j], lo[j]], axis=0), PLAIN)

    def where(i, j, m):
        off = jnp.int32(offsets[0])
        for at, o in enumerate(offsets[1:], 1):
            off = jnp.where(j == at, o, off)
        return i, lax.rem(m[1] + off, 4)

    ins = [pl.BlockSpec((WIDE, 2 * piece), where)] + [ONCHIP] * (len(flat_v) + len(flat_y))
    operands, aliases = [meta, block, *map(resident, flat_v), *flat_y], {}
    if before is not None:
        aliases = {len(operands): 0}
        ins.append(pl.BlockSpec(memory_space=pl.ANY))
        operands.append(before)
    scratch = [pltpu.VMEM((len(ys), order, 2 * piece), BF16)] * 2
    return call(
        kernel, (rows // WIDE, len(ys)), ins, [(pl.BlockSpec((WIDE, 2 * piece), where), shape(rows, cols))],
        scratch, operands, aliases, flops=6 * rows * order * 2 * piece * len(ys),
    )[0]


def near_sum(mine, theirs):
    received = shifted(theirs, "k", 1)
    both = [m + r for m, r in zip(mine, received)]
    near = shifted(both[1], "y", 1), shifted(both[3], "y", -1), shifted(both[2], "y", 2)
    return both[0] + near[0] + near[1] + near[2]


def near_sum_behind(mine, theirs, deep):
    both = mine + shifted(theirs, "k", 1)

    def with_rest(at):
        return jnp.concatenate([both[at * deep : (at + 1) * deep], both[4 * deep :]])

    near = shifted(with_rest(1), "y", 1), shifted(both[3 * deep :], "y", -1), shifted(with_rest(2), "y", 2)
    return with_rest(0) + near[0] + near[1] + near[2]


def doubled(total):
    return total + shifted(total, "zh", 1)


def from_everyone(piece, axes):
    peers = lax.axis_size(axes)
    return lax.all_to_all(jnp.broadcast_to(piece[None], (peers, *piece.shape)), axes, 0, 0, tiled=True)


def shards(vectors, reflectors, triangles):
    own, tri = reflectors[0], triangles[0]
    core, y, z, x = (lax.axis_index(a) for a in ("k", "y", "zl", "x"))
    places = []
    for p in range(8):
        pz, px = divmod(p, 4)
        dx = lax.rem(px - x + 4, 4)
        same = jnp.where(dx == 0, 0, jnp.where(dx == 3, 1, jnp.where(dx == 1, 2, 4)))
        cross = jnp.where(dx == 0, 3, jnp.where(dx == 3, 5, jnp.where(dx == 1, 6, 7)))
        places.append(jnp.where(pz == z, same, cross))
    meta = jnp.stack([core, y, x, z, *places]).astype(jnp.int32)
    return body(meta, vectors, own, tri)


def body(meta, vectors, own, tri):
    half = own.shape[0] // 2
    split = held(meta, vectors)
    upper, lower = own[:half], own[half:]
    left0, right1 = shifted(upper, "x", 1), shifted(lower, "x", -1)
    across = shifted(own, "zl", 1)
    left1, right0 = shifted(lower, "x", 1), shifted(upper, "x", -1)
    far = shifted(left0, "x", 1), shifted(right1, "x", -1)
    left, right = (left0, left1), (right0, right1)
    across_left, across_right = shifted(across, "x", 1), shifted(across, "x", -1)
    across_far = shifted(far[0], "zl", 1), shifted(far[1], "zl", 1)

    m0, t0, h0, l0 = panel_products(meta, split, [(own,)])
    sum0 = near_sum(m0, t0)
    m1, t1, h1, l1 = panel_products(meta, split, [left, right, (across,)])
    deep = m1.shape[1]
    m1, t1 = inner_products(meta, [(own,), left, (across,), far], m1, t1)
    sum1 = near_sum_behind(m1, t1, deep)
    gsum = doubled(sum1[deep:])
    early = doubled(jnp.concatenate([sum0, sum1[:deep]]))
    width = tri.shape[0]
    part = lax.dynamic_slice_in_dim(tri, meta[0] * (width // 2), width // 2)
    gall = from_everyone(jnp.concatenate([gsum, part]), ("zl", "x"))
    inner = coupling(meta, gall, shifted(gall, "k", 1))
    m2, t2, h2, l2 = panel_products(meta, split, [far, (across_left,), (across_right,), across_far])
    late = doubled(near_sum(m2, t2))
    ys = solved(meta, (early, late), inner)

    bases = (h0, l0), (h1, l1), (h2, l2)
    ahead, behind = shifted(ys, "y", -1), shifted(ys, "y", 1)
    out = updated(meta, vectors, bases, [(ys, shifted(ys, "k", 1))], (0,), None)
    top = ys.shape[0] // 2
    away = shifted(ahead[:top], "y", -1), shifted(behind[top:], "y", 1)
    side = [(v, shifted(v, "k", 1)) for v in (ahead, behind)]
    out = updated(meta, vectors, bases, side, (1, 3), out)
    away = jnp.concatenate(away)
    return updated(meta, vectors, bases, [(away, shifted(away, "k", 1))], (2,), out)


def solution(mesh):
    torus = Mesh(mesh.devices.reshape(4, 2, 2, 2, 4), ROW + COL)
    return jax.shard_map(
        shards,
        mesh=torus,
        in_specs=(P(ROW, COL), P(COL, ROW, None), P(COL, None, None)),
        out_specs=P(ROW, COL),
        check_vma=False,
    )
```

time: 219 us -> 201 us (0.918)
  Pallas kernels: 82.8 us -> 59.2 us
  blocking collectives: 17.4 us -> 0 us
  local copies, waits for them, and re-layouts: 10.2 us -> 19.7 us
  starting transfers between devices: 44.5 us -> 52.5 us
  waiting for transfers between devices: 57.9 us -> 63.9 us
    pallas_call x9 -> x10, Pallas kernels: 82.8 us -> 59.2 us  [call(): pl.pallas_call(kernel, grid_spec=pltpu.PrefetchScalarGridSpec(num_scalar_...]
    all_to_all x1 -> x0, blocking collectives: 17.4 us -> none  [body(): lax.all_to_all(ginner.reshape(8, *ginner.shape[2:]), ('y', 'k'), 0, 0, ti...]
    unnamed x35 -> x65, local copies, waits for them, and re-layouts: 6.07 us -> 15.3 us
    ppermute x35, starting transfers between devices: 40.6 us -> 48.2 us  [shifted(): lax.ppermute(value, axis, [(i, (i + by) % peers) for i in range(peers)])]
    ppermute x35, waiting for transfers between devices: 57.9 us -> 63.9 us  [shifted(): lax.ppermute(value, axis, [(i, (i + by) % peers) for i in range(peers)])]
  transfers between devices with their start and end apart: 36 -> 36, of which waited for: 12 -> 10; matrix products, arithmetic and copies ran while one was open for 4% -> 5% of each run, Pallas kernels for 28% -> 21%
where the time goes in v1:
time: 201 us
  waiting for transfers between devices  63.9 us (32%)
  Pallas kernels  59.2 us (29%)
  starting transfers between devices  52.5 us (26%)
  local copies, waits for them, and re-layouts  19.7 us (10%)
  other arithmetic  4.8 us (2%)
    ppermute x35, waiting for transfers between devices, shifted(): lax.ppermute(value, axis, [(i, (i + by) % peers) for i in range(peers)])  63.9 us
    pallas_call x10, Pallas kernels, call(): pl.pallas_call(kernel, grid_spec=pltpu.PrefetchScalarGridSpec(num_scalar_...  59.2 us
    ppermute x35, starting transfers between devices, shifted(): lax.ppermute(value, axis, [(i, (i + by) % peers) for i in range(peers)])  48.2 us
    unnamed x65, local copies, waits for them, and re-layouts  15.3 us
    all_to_all x1, starting transfers between devices, from_everyone(): lax.all_to_all(jnp.broadcast_to(piece[None], (peers, *piece.shape)), axes...  4.25 us
  transfers between devices with their start and end apart: 36, of which 10 were waited for; matrix products, arithmetic and copies ran while one was open for 5% of the time, Pallas kernels for 21%

profile of v1, /device:TPU:1, one launch (start us, length us, event | category | flops | bytes accessed | tf_op | source)
XLA Modules:
  0.0 200.5 jit_solution(13092753070696996717)
XLA Ops:
  10.1 8.7 %collective-permute-done.refs_0_.refs_1_ = f32[1024,128]{1,0:T(8,128)} collective-permute-done((f32[1024,128]{1,0:T(8,128)}, f32[1024,128]{1,0:T(8,128)}, u32[]{:S(2)}, u32[]{:S(2)}) %collective-permute-start) | collective-permute-done | bytes 524320 | tf_op jit(solution)/shard_map/ppermute | solution.py:19
  18.8 2.7 %collective-permute-start.6 = (f32[1024,128]{1,0:T(8,128)}, f32[1024,128]{1,0:T(8,128)S(1)}, u32[]{:S(2)}, u32[]{:S(2)}) collective-permute-start(f32[1024,128]{1,0:T(8,128)} %collective-permute-done.3.refs_3_), channel_id=1, source_target_pairs={{0,3},{1,0},{2,1},{3,2},{4,7},{5,4},{6,5},{7,6},{8,11},{9,8},{10,9... | collective-permute-start | bytes 1572872 | tf_op jit(solution)/shard_map/ppermute | solution.py:19
  21.6 3.4 %copy-done.2 = f32[2048,1024]{1,0:T(8,128)S(1)} copy-done((f32[2048,1024]{1,0:T(8,128)S(1)}, f32[2048,1024]{1,0:T(8,128)}, u32[]{:S(2)}) %copy-start.2) | copy-done | bytes 8388632
  27.0 3.0 %collective-permute-done.1.refs_1_.refs_2_ = f32[1024,128]{1,0:T(8,128)S(1)} collective-permute-done((f32[1024,128]{1,0:T(8,128)}, f32[1024,128]{1,0:T(8,128)S(1)}, u32[]{:S(2)}, u32[]{:S(2)}) %collective-permute-start.1) | collective-permute-done | bytes 524320 | tf_op jit(solution)/shard_map/ppermute | solution.py:19
  33.7 8.3 %shard_map.39 = (f32[4,384,128]{2,1,0:T(8,128)S(1)}, f32[4,384,128]{2,1,0:T(8,128)S(1)}, bf16[2048,384]{1,0:T(8,128)(2,1)S(1)}, bf16[2048,384]{1,0:T(8,128)(2,1)S(1)}) custom-call(s32[12]{0:T(128)S(1)} %stack.51.m, bf16[2048,1024]{1,0:T(8,128)(2,1)S(1)} %get-tuple-element.25.xh_ref, bf16[2048,1024]{1,0:T(8,128)(2,1)S(1)} %get-tuple-element.26.xl_ref, ...), custom_call_target="tpu_custom_call" | custom-call | flops 4831838208 | bytes 18874368 | tf_op jit(solution)/shard_map/pallas_call | solution.py:42
  42.1 5.3 %shard_map.41 = (f32[1760,128]{1,0:T(8,128)S(1)}, f32[1760,128]{1,0:T(8,128)S(1)}) custom-call(s32[12]{0:T(128)S(1)} %stack.51.m, f32[2048,128]{1,0:T(8,128)S(1)} %bitcast.50, f32[1024,128]{1,0:T(8,128)} %collective-permute-done.refs_0_.refs_1_, f32[1024,128]{1,0:T(8,128)S(1)} %copy-done.24, f32[2048,128]{1,0:T(8,128)S(1)} %collective-permute-done.4.refs_4_.refs_3_, ...), custom_call_target="tpu_custom_call" | custom-call | flops 1006632960 | bytes 3932160 | tf_op jit(solution)/shard_map/pallas_call | solution.py:42
  47.4 3.5 %collective-permute-start.15 = (f32[1760,128]{1,0:T(8,128)S(1)}, f32[1760,128]{1,0:T(8,128)S(1)}, u32[]{:S(2)}, u32[]{:S(2)}) collective-permute-start(f32[1760,128]{1,0:T(8,128)S(1)} %get-tuple-element.38), channel_id=1, source_target_pairs={{0,8},{8,0},{1,9},{9,1},{2,10},{10,2},{3,11},{11,3},{4,12},{12,4},... | collective-permute-start | bytes 2703368 | tf_op jit(solution)/shard_map/ppermute | solution.py:19
  59.0 4.6 %collective-permute-done.16 = f32[608,128]{1,0:T(8,128)S(1)} collective-permute-done((f32[608,128]{1,0:T(8,128)S(1)}, f32[608,128]{1,0:T(8,128)S(1)}, u32[]{:S(2)}, u32[]{:S(2)}) %collective-permute-start.16) | collective-permute-done | bytes 311328 | tf_op jit(solution)/shard_map/ppermute | solution.py:19
  63.6 7.7 %collective-permute-done.18 = f32[608,128]{1,0:T(8,128)S(1)} collective-permute-done((f32[608,128]{1,0:T(8,128)S(1)}, f32[608,128]{1,0:T(8,128)S(1)}, u32[]{:S(2)}, u32[]{:S(2)}) %collective-permute-start.18) | collective-permute-done | bytes 311328 | tf_op jit(solution)/shard_map/ppermute | solution.py:19
  72.1 3.4 %collective-permute-start.25 = (f32[224,128]{1,0:T(8,128)}, f32[224,128]{1,0:T(8,128)}, u32[]{:S(2)}, u32[]{:S(2)}) collective-permute-start(f32[224,128]{1,0:T(8,128)} %slice.60), channel_id=1, source_target_pairs={{0,16},{16,0},{1,17},{17,1},{2,18},{18,2},{3,19},{19,3},{4,20},{20... | collective-permute-start | bytes 344072 | tf_op jit(solution)/shard_map/ppermute | solution.py:19
  75.5 15.7 %collective-permute-done.25 = f32[224,128]{1,0:T(8,128)} collective-permute-done((f32[224,128]{1,0:T(8,128)}, f32[224,128]{1,0:T(8,128)}, u32[]{:S(2)}, u32[]{:S(2)}) %collective-permute-start.25) | collective-permute-done | bytes 114720 | tf_op jit(solution)/shard_map/ppermute | solution.py:19
  93.2 4.3 %all-to-all-start = ((f32[8,288,128]{2,1,0:T(8,128)}), f32[8,288,128]{2,1,0:T(8,128)}, u32[]{:S(2)}, u32[]{:S(2)}) async-start(f32[8,288,128]{2,1,0:T(8,128)} %broadcast_in_dim.2), calls=%async_computation | async-start | bytes 2359296 | tf_op jit(solution)/shard_map/all_to_all | solution.py:343
  104.0 11.3 %shard_map.40 = (f32[4,512,128]{2,1,0:T(8,128)S(1)}, f32[4,512,128]{2,1,0:T(8,128)}, bf16[2048,512]{1,0:T(8,128)(2,1)S(1)}, bf16[2048,512]{1,0:T(8,128)(2,1)S(1)}) custom-call(s32[12]{0:T(128)S(1)} %stack.51.m, bf16[2048,1024]{1,0:T(8,128)(2,1)S(1)} %copy-done.15, bf16[2048,1024]{1,0:T(8,128)(2,1)S(1)} %copy-done.17, f32[1024,128]{1,0:T(8,128)S(1)} %copy-done.20, ...), custom_call_target="tpu_custom_call" | custom-call | flops 6442450944 | bytes 25165824 | tf_op jit(solution)/shard_map/pallas_call | solution.py:42
  117.8 4.0 %shard_map.38 = (f32[4,128,128]{2,1,0:T(8,128)S(1)}, f32[4,128,128]{2,1,0:T(8,128)}, bf16[2048,128]{1,0:T(8,128)(2,1)S(1)}, bf16[2048,128]{1,0:T(8,128)(2,1)S(1)}) custom-call(s32[12]{0:T(128)S(1)} %stack.51.m, bf16[2048,1024]{1,0:T(8,128)(2,1)S(1)} %copy-done.15, bf16[2048,1024]{1,0:T(8,128)(2,1)S(1)} %copy-done.17, f32[2048,128]{1,0:T(8,128)S(1)} %bitcast.51), custom_call_target="tpu_custom_call" | custom-call | flops 1610612736 | bytes 6291456 | tf_op jit(solution)/shard_map/pallas_call | solution.py:42
  135.4 3.1 %collective-permute-done.21 = f32[512,128]{1,0:T(8,128)S(1)} collective-permute-done((f32[512,128]{1,0:T(8,128)S(1)}, f32[512,128]{1,0:T(8,128)S(1)}, u32[]{:S(2)}, u32[]{:S(2)}) %collective-permute-start.21) | collective-permute-done | bytes 262176 | tf_op jit(solution)/shard_map/ppermute | solution.py:19
  138.5 5.9 %collective-permute-done.23 = f32[512,128]{1,0:T(8,128)S(1)} collective-permute-done((f32[512,128]{1,0:T(8,128)S(1)}, f32[512,128]{1,0:T(8,128)S(1)}, u32[]{:S(2)}, u32[]{:S(2)}) %collective-permute-start.23) | collective-permute-done | bytes 262176 | tf_op jit(solution)/shard_map/ppermute | solution.py:19
  145.8 7.6 %collective-permute-done.24 = f32[512,128]{1,0:T(8,128)S(1)} collective-permute-done((f32[512,128]{1,0:T(8,128)S(1)}, f32[512,128]{1,0:T(8,128)S(1)}, u32[]{:S(2)}, u32[]{:S(2)}) %collective-permute-start.24) | collective-permute-done | bytes 262176 | tf_op jit(solution)/shard_map/ppermute | solution.py:19
  155.9 3.8 %shard_map.43.refs_6_ = f32[1024,128]{1,0:T(8,128)S(1)} custom-call(s32[12]{0:T(128)S(1)} %stack.51.m, f32[512,128]{1,0:T(8,128)S(1)} %fusion.17.refs_0_, f32[512,128]{1,0:T(8,128)S(1)} %add.141.refs_1_, bf16[8,1024,128]{2,1,0:T(8,128)(2,1)S(1)} %get-tuple-element.41.refs_2_, bf16[8,1024,128]{2,1,0:T(8,128)(2,1)S(1)} %get-tuple-element.42.refs_3_, ...), custom_call_target="tpu_custom_call" | custom-call | flops 805306368 | bytes 3145728 | tf_op jit(solution)/shard_map/pallas_call | solution.py:42
  161.2 3.2 %collective-permute-start.34 = (f32[1024,128]{1,0:T(8,128)S(1)}, f32[1024,128]{1,0:T(8,128)S(1)}, u32[]{:S(2)}, u32[]{:S(2)}) collective-permute-start(f32[1024,128]{1,0:T(8,128)S(1)} %shard_map.43.refs_6_), channel_id=1, source_target_pairs={{0,8},{8,0},{1,9},{9,1},{2,10},{10,2},{3,11},{11,3},{4,12},{12,4},... | collective-permute-start | bytes 1572872 | tf_op jit(solution)/shard_map/ppermute | solution.py:19
  164.4 6.3 %collective-permute-done.27.refs_6_ = f32[1024,128]{1,0:T(8,128)S(1)} collective-permute-done((f32[1024,128]{1,0:T(8,128)S(1)}, f32[1024,128]{1,0:T(8,128)S(1)}, u32[]{:S(2)}, u32[]{:S(2)}) %collective-permute-start.27) | collective-permute-done | bytes 524320 | tf_op jit(solution)/shard_map/ppermute | solution.py:19
  172.4 4.3 %collective-permute-start.32 = (f32[1024,128]{1,0:T(8,128)S(1)}, f32[1024,128]{1,0:T(8,128)S(1)}, u32[]{:S(2)}, u32[]{:S(2)}) collective-permute-start(f32[1024,128]{1,0:T(8,128)S(1)} %collective-permute-done.27.refs_6_), channel_id=1, source_target_pairs={{0,8},{8,0},{1,9},{9,1},{2,10},{10,2},{3,11},{11,3},{4,12},{12,4},... | collective-permute-start | bytes 1572872 | tf_op jit(solution)/shard_map/ppermute | solution.py:19
  176.9 5.9 %shard_map.44.refs_10_ = f32[2048,1024]{1,0:T(8,128)} custom-call(s32[12]{0:T(128)S(1)} %stack.51.m, f32[2048,1024]{1,0:T(8,128)S(1)} %bitcast.48, bf16[2048,128]{1,0:T(8,128)(2,1)S(1)} %copy-done.11, bf16[2048,128]{1,0:T(8,128)(2,1)S(1)} %copy-done.13, bf16[2048,384]{1,0:T(8,128)(2,1)S(1)} %copy-done.6, bf16[2048,384]{1,0:T(8,128)(2,1)S(1)} %copy-done.8, ...), custom_call_target="tpu_custom_call" | custom-call | flops 3221225472 | bytes 12582912 | tf_op jit(solution)/shard_map/pallas_call | solution.py:42
  184.3 10.3 %shard_map.45.refs_8_ = f32[2048,1024]{1,0:T(8,128)} custom-call(s32[12]{0:T(128)S(1)} %stack.51.m, f32[2048,1024]{1,0:T(8,128)S(1)} %bitcast.48, bf16[2048,128]{1,0:T(8,128)(2,1)S(1)} %copy-done.11, bf16[2048,128]{1,0:T(8,128)(2,1)S(1)} %copy-done.13, bf16[2048,384]{1,0:T(8,128)(2,1)S(1)} %copy-done.6, ...), custom_call_target="tpu_custom_call", output_to_operand_aliasing={{}: (12, {})} | custom-call | flops 6442450944 | bytes 25165824 | tf_op jit(solution)/shard_map/pallas_call | solution.py:42
  194.7 5.9 %shard_map.46 = f32[2048,1024]{1,0:T(8,128)} custom-call(s32[12]{0:T(128)S(1)} %stack.51.m, f32[2048,1024]{1,0:T(8,128)S(1)} %bitcast.48, bf16[2048,128]{1,0:T(8,128)(2,1)S(1)} %copy-done.11, bf16[2048,128]{1,0:T(8,128)(2,1)S(1)} %copy-done.13, bf16[2048,384]{1,0:T(8,128)(2,1)S(1)} %copy-done.6, ...), custom_call_target="tpu_custom_call", output_to_operand_aliasing={{}: (10, {})} | custom-call | flops 3221225472 | bytes 12582912 | tf_op jit(solution)/shard_map/pallas_call | solution.py:42
  (148 shorter events, 57.9 us)
Async XLA Ops:
  0.0 31.6 %collective-permute-start.4 = (f32[2048,128]{1,0:T(8,128)}, f32[2048,128]{1,0:T(8,128)S(1)}, u32[]{:S(2)}, u32[]{:S(2)}) collective-permute-start(f32[2048,128]{1,0:T(8,128)} %bitcast.49), channel_id=1, source_target_pairs={{0,4},{4,0},{1,5},{5,1},{2,6},{6,2},{3,7},{7,3},{8,12},{12,8},{9,1... | collective-permute-start | bytes 3145736 | tf_op jit(solution)/shard_map/ppermute | solution.py:19
  4.8 14.1 %collective-permute-start = (f32[1024,128]{1,0:T(8,128)}, f32[1024,128]{1,0:T(8,128)}, u32[]{:S(2)}, u32[]{:S(2)}) collective-permute-start(f32[1024,128]{1,0:T(8,128)} %get-tuple-element.49), channel_id=1, source_target_pairs={{0,1},{1,2},{2,3},{3,0},{4,5},{5,6},{6,7},{7,4},{8,9},{9,10},{10,1... | collective-permute-start | bytes 1572872 | tf_op jit(solution)/shard_map/ppermute | solution.py:19
  6.0 12.8 %collective-permute-start.3 = (f32[1024,128]{1,0:T(8,128)}, f32[1024,128]{1,0:T(8,128)}, u32[]{:S(2)}, u32[]{:S(2)}) collective-permute-start(f32[1024,128]{1,0:T(8,128)} %get-tuple-element.48), channel_id=1, source_target_pairs={{0,3},{1,0},{2,1},{3,2},{4,7},{5,4},{6,5},{7,6},{8,11},{9,8},{10,9... | collective-permute-start | bytes 1572872 | tf_op jit(solution)/shard_map/ppermute | solution.py:19
  7.5 22.5 %collective-permute-start.1 = (f32[1024,128]{1,0:T(8,128)}, f32[1024,128]{1,0:T(8,128)S(1)}, u32[]{:S(2)}, u32[]{:S(2)}) collective-permute-start(f32[1024,128]{1,0:T(8,128)} %get-tuple-element.48), channel_id=1, source_target_pairs={{0,1},{1,2},{2,3},{3,0},{4,5},{5,6},{6,7},{7,4},{8,9},{9,10},{10,1... | collective-permute-start | bytes 1572872 | tf_op jit(solution)/shard_map/ppermute | solution.py:19
  7.5 23.3 %collective-permute-start.2 = (f32[1024,128]{1,0:T(8,128)}, f32[1024,128]{1,0:T(8,128)S(1)}, u32[]{:S(2)}, u32[]{:S(2)}) collective-permute-start(f32[1024,128]{1,0:T(8,128)} %get-tuple-element.49), channel_id=1, source_target_pairs={{0,3},{1,0},{2,1},{3,2},{4,7},{5,4},{6,5},{7,6},{8,11},{9,8},{10,9... | collective-permute-start | bytes 1572872 | tf_op jit(solution)/shard_map/ppermute | solution.py:19
  18.8 23.2 %collective-permute-start.5 = (f32[1024,128]{1,0:T(8,128)}, f32[1024,128]{1,0:T(8,128)S(1)}, u32[]{:S(2)}, u32[]{:S(2)}) collective-permute-start(f32[1024,128]{1,0:T(8,128)} %collective-permute-done.refs_0_.refs_1_), channel_id=1, source_target_pairs={{0,1},{1,2},{2,3},{3,0},{4,5},{5,6},{6,7},{7,4},{8,9},{9,10},{10,1... | collective-permute-start | bytes 1572872 | tf_op jit(solution)/shard_map/ppermute | solution.py:19
  18.8 23.2 %collective-permute-start.6 = (f32[1024,128]{1,0:T(8,128)}, f32[1024,128]{1,0:T(8,128)S(1)}, u32[]{:S(2)}, u32[]{:S(2)}) collective-permute-start(f32[1024,128]{1,0:T(8,128)} %collective-permute-done.3.refs_3_), channel_id=1, source_target_pairs={{0,3},{1,0},{2,1},{3,2},{4,7},{5,4},{6,5},{7,6},{8,11},{9,8},{10,9... | collective-permute-start | bytes 1572872 | tf_op jit(solution)/shard_map/ppermute | solution.py:19
  50.9 46.6 %collective-permute-start.7 = (f32[2048,128]{1,0:T(8,128)S(1)}, f32[2048,128]{1,0:T(8,128)}, u32[]{:S(2)}, u32[]{:S(2)}) collective-permute-start(f32[2048,128]{1,0:T(8,128)S(1)} %collective-permute-done.4.refs_4_.refs_3_), channel_id=1, source_target_pairs={{0,1},{1,2},{2,3},{3,0},{4,5},{5,6},{6,7},{7,4},{8,9},{9,10},{10,1... | collective-permute-start | bytes 3145736 | tf_op jit(solution)/shard_map/ppermute | solution.py:19
  51.4 46.1 %collective-permute-start.8 = (f32[2048,128]{1,0:T(8,128)S(1)}, f32[2048,128]{1,0:T(8,128)}, u32[]{:S(2)}, u32[]{:S(2)}) collective-permute-start(f32[2048,128]{1,0:T(8,128)S(1)} %collective-permute-done.4.refs_4_.refs_3_), channel_id=1, source_target_pairs={{0,3},{1,0},{2,1},{3,2},{4,7},{5,4},{6,5},{7,6},{8,11},{9,8},{10,9... | collective-permute-start | bytes 3145736 | tf_op jit(solution)/shard_map/ppermute | solution.py:19
  55.1 16.1 %collective-permute-start.18 = (f32[608,128]{1,0:T(8,128)S(1)}, f32[608,128]{1,0:T(8,128)S(1)}, u32[]{:S(2)}, u32[]{:S(2)}) collective-permute-start(f32[608,128]{1,0:T(8,128)S(1)} %get-tuple-element.57), channel_id=1, source_target_pairs={{0,64},{32,96},{64,0},{96,32},{1,65},{33,97},{65,1},{97,33},{2,66}... | collective-permute-start | bytes 933896 | tf_op jit(solution)/shard_map/ppermute | solution.py:19
  57.8 13.5 %collective-permute-start.17 = (f32[608,128]{1,0:T(8,128)S(1)}, f32[608,128]{1,0:T(8,128)S(1)}, u32[]{:S(2)}, u32[]{:S(2)}) collective-permute-start(f32[608,128]{1,0:T(8,128)S(1)} %slice.57), channel_id=1, source_target_pairs={{0,96},{32,0},{64,32},{96,64},{1,97},{33,1},{65,33},{97,65},{2,98}... | collective-permute-start | bytes 933896 | tf_op jit(solution)/shard_map/ppermute | solution.py:19
  63.6 33.9 %collective-permute-start.9 = (f32[1024,128]{1,0:T(8,128)S(1)}, f32[1024,128]{1,0:T(8,128)}, u32[]{:S(2)}, u32[]{:S(2)}) collective-permute-start(f32[1024,128]{1,0:T(8,128)S(1)} %collective-permute-done.5.refs_0_.refs_4_), channel_id=1, source_target_pairs={{0,4},{4,0},{1,5},{5,1},{2,6},{6,2},{3,7},{7,3},{8,12},{12,8},{9,1... | collective-permute-start | bytes 1572872 | tf_op jit(solution)/shard_map/ppermute | solution.py:19
  71.3 26.2 %collective-permute-start.10 = (f32[1024,128]{1,0:T(8,128)S(1)}, f32[1024,128]{1,0:T(8,128)}, u32[]{:S(2)}, u32[]{:S(2)}) collective-permute-start(f32[1024,128]{1,0:T(8,128)S(1)} %collective-permute-done.6.refs_1_.refs_5_), channel_id=1, source_target_pairs={{0,4},{4,0},{1,5},{5,1},{2,6},{6,2},{3,7},{7,3},{8,12},{12,8},{9,1... | collective-permute-start | bytes 1572872 | tf_op jit(solution)/shard_map/ppermute | solution.py:19
  72.1 19.1 %collective-permute-start.25 = (f32[224,128]{1,0:T(8,128)}, f32[224,128]{1,0:T(8,128)}, u32[]{:S(2)}, u32[]{:S(2)}) collective-permute-start(f32[224,128]{1,0:T(8,128)} %slice.60), channel_id=1, source_target_pairs={{0,16},{16,0},{1,17},{17,1},{2,18},{18,2},{3,19},{19,3},{4,20},{20... | collective-permute-start | bytes 344072 | tf_op jit(solution)/shard_map/ppermute | solution.py:19
  93.2 30.2 %all-to-all-start = ((f32[8,288,128]{2,1,0:T(8,128)}), f32[8,288,128]{2,1,0:T(8,128)}, u32[]{:S(2)}, u32[]{:S(2)}) async-start(f32[8,288,128]{2,1,0:T(8,128)} %broadcast_in_dim.2), calls=%async_computation | async-start | bytes 2359296 | tf_op jit(solution)/shard_map/all_to_all | solution.py:343
  115.3 13.4 %collective-permute-start.20 = (f32[4,512,128]{2,1,0:T(8,128)}, f32[4,512,128]{2,1,0:T(8,128)}, u32[]{:S(2)}, u32[]{:S(2)}) collective-permute-start(f32[4,512,128]{2,1,0:T(8,128)} %get-tuple-element.40), channel_id=1, source_target_pairs={{0,8},{8,0},{1,9},{9,1},{2,10},{10,2},{3,11},{11,3},{4,12},{12,4},... | collective-permute-start | bytes 3145736 | tf_op jit(solution)/shard_map/ppermute | solution.py:19
  123.5 29.9 %collective-permute-start.26 = (f32[8,288,128]{2,1,0:T(8,128)}, f32[8,288,128]{2,1,0:T(8,128)S(1)}, u32[]{:S(2)}, u32[]{:S(2)}) collective-permute-start(f32[8,288,128]{2,1,0:T(8,128)} %all-to-all-done.a_ref), channel_id=1, source_target_pairs={{0,8},{8,0},{1,9},{9,1},{2,10},{10,2},{3,11},{11,3},{4,12},{12,4},... | collective-permute-start | bytes 3538952 | tf_op jit(solution)/shard_map/ppermute | solution.py:19
  133.1 11.3 %collective-permute-start.23 = (f32[512,128]{1,0:T(8,128)S(1)}, f32[512,128]{1,0:T(8,128)S(1)}, u32[]{:S(2)}, u32[]{:S(2)}) collective-permute-start(f32[512,128]{1,0:T(8,128)S(1)} %get-tuple-element.46), channel_id=1, source_target_pairs={{0,64},{32,96},{64,0},{96,32},{1,65},{33,97},{65,1},{97,33},{2,66}... | collective-permute-start | bytes 786440 | tf_op jit(solution)/shard_map/ppermute | solution.py:19
  159.7 11.1 %collective-permute-start.27 = (f32[1024,128]{1,0:T(8,128)S(1)}, f32[1024,128]{1,0:T(8,128)S(1)}, u32[]{:S(2)}, u32[]{:S(2)}) collective-permute-start(f32[1024,128]{1,0:T(8,128)S(1)} %shard_map.43.refs_6_), channel_id=1, source_target_pairs={{0,96},{32,0},{64,32},{96,64},{1,97},{33,1},{65,33},{97,65},{2,98}... | collective-permute-start | bytes 1572872 | tf_op jit(solution)/shard_map/ppermute | solution.py:19
  161.2 15.6 %collective-permute-start.34 = (f32[1024,128]{1,0:T(8,128)S(1)}, f32[1024,128]{1,0:T(8,128)S(1)}, u32[]{:S(2)}, u32[]{:S(2)}) collective-permute-start(f32[1024,128]{1,0:T(8,128)S(1)} %shard_map.43.refs_6_), channel_id=1, source_target_pairs={{0,8},{8,0},{1,9},{9,1},{2,10},{10,2},{3,11},{11,3},{4,12},{12,4},... | collective-permute-start | bytes 1572872 | tf_op jit(solution)/shard_map/ppermute | solution.py:19
  170.8 11.9 %collective-permute-start.28 = (f32[512,128]{1,0:T(8,128)S(1)}, f32[512,128]{1,0:T(8,128)S(1)}, u32[]{:S(2)}, u32[]{:S(2)}) collective-permute-start(f32[512,128]{1,0:T(8,128)S(1)} %slice.61), channel_id=1, source_target_pairs={{0,96},{32,0},{64,32},{96,64},{1,97},{33,1},{65,33},{97,65},{2,98}... | collective-permute-start | bytes 786440 | tf_op jit(solution)/shard_map/ppermute | solution.py:19
  170.9 11.8 %collective-permute-start.30 = (f32[512,128]{1,0:T(8,128)S(1)}, f32[512,128]{1,0:T(8,128)S(1)}, u32[]{:S(2)}, u32[]{:S(2)}) collective-permute-start(f32[512,128]{1,0:T(8,128)S(1)} %slice.62), channel_id=1, source_target_pairs={{0,32},{32,64},{64,96},{96,0},{1,33},{33,65},{65,97},{97,1},{2,34}... | collective-permute-start | bytes 786440 | tf_op jit(solution)/shard_map/ppermute | solution.py:19
  172.4 11.9 %collective-permute-start.32 = (f32[1024,128]{1,0:T(8,128)S(1)}, f32[1024,128]{1,0:T(8,128)S(1)}, u32[]{:S(2)}, u32[]{:S(2)}) collective-permute-start(f32[1024,128]{1,0:T(8,128)S(1)} %collective-permute-done.27.refs_6_), channel_id=1, source_target_pairs={{0,8},{8,0},{1,9},{9,1},{2,10},{10,2},{3,11},{11,3},{4,12},{12,4},... | collective-permute-start | bytes 1572872 | tf_op jit(solution)/shard_map/ppermute | solution.py:19
  182.8 11.9 %collective-permute-start.31 = (f32[1024,128]{1,0:T(8,128)S(1)}, f32[1024,128]{1,0:T(8,128)S(1)}, u32[]{:S(2)}, u32[]{:S(2)}) collective-permute-start(f32[1024,128]{1,0:T(8,128)S(1)} %constant_dynamic-update-slice_fusion.refs_6_), channel_id=1, source_target_pairs={{0,8},{8,0},{1,9},{9,1},{2,10},{10,2},{3,11},{11,3},{4,12},{12,4},... | collective-permute-start | bytes 1572872 | tf_op jit(solution)/shard_map/ppermute | solution.py:19
  (44 other events, 525.6 us)
